TPU v7x, 32 devices: a whole 2x2x4 slice. The times are simulated.
32 devices in a mesh: blk: 8 (over z, y), feat: 4 (over x, core).
Axes of the slice: x: 2, y: 2, z: 4, core: 2. Of those that a mesh axis runs over, the one named last changes fastest.
Arguments:
- node_feats: bfloat16 [65536, 256], P('blk', 'feat'), may hold values from -6 to 6
- tile_rows: int32 [64, 128], P('blk'), may hold values from 0 to 63, as said below
- tile_cols: int32 [64, 128], P('blk'), may hold values from 0 to 63, as said below
- tile_values: bfloat16 [64, 128, 128, 128], P('blk'), may hold values from 0 to 0.1, as said below
- eps_self: float32 [1], replicated, may hold values from -0.5 to 0.5
- w_one: bfloat16 [256, 256], P(None, 'feat'), may hold values from -0.375 to 0.375
- b_one: bfloat16 [256], P('feat'), may hold values from -3 to 3
- w_two: bfloat16 [256, 256], P('feat'), may hold values from -0.375 to 0.375
- b_two: bfloat16 [256], P('feat'), may hold values from -3 to 3
Outputs:
- layer_out: bfloat16 [65536, 256], P('blk', 'feat')
Inputs may be any that keep to these rules, and one draw needn't show every extreme that they name: `tile_rows`: every entry names a row of tiles inside a node block: 0 to 63; within one row of the lists no pair (tile_rows, tile_cols) repeats; every row of tiles of every node block holds at least one nonzero tile. `tile_cols`: every entry names a column of tiles inside a source block: 0 to 63; every node block has exactly 128 tiles in each source block; every column of tiles of every source block is used by at least one node block. `tile_values`: edge weights are 0 or positive and below 0.1.
All inputs are finite; a program needn't handle non-finite values.
Results may differ from a plain program's by a relative error of at most 0.01.
Values may be sent and summed in bfloat16 or wider, within the bound.
A program may use at most 192 MiB of HBM per device.

v0:
```python
import jax
import jax.numpy as jnp
from jax import lax
from jax.sharding import PartitionSpec as P


def on_device(node_feats, tile_rows, tile_cols, tile_values, eps_self, w_one, b_one, w_two, b_two):
    rows_dev = node_feats.shape[0]
    feat_width = node_feats.shape[1]
    tile_size = tile_values.shape[2]
    blocks = tile_rows.shape[0]
    row_tiles = rows_dev // tile_size
    tile_index = jnp.arange(row_tiles, dtype=jnp.int32)
    row_marks_all = (tile_rows[:, :, None] == tile_index[None, None, :]).astype(jnp.float32)
    col_marks_all = (tile_cols[:, :, None] == tile_index[None, None, :]).astype(jnp.bfloat16)

    def absorb(running, segment, begin):
        piece_len = segment.shape[0]
        if piece_len % rows_dev == 0:
            src_count = piece_len // rows_dev
        else:
            src_count = piece_len // rows_dev + 2
        first_src = begin // rows_dev
        shift_rows = (begin - first_src * rows_dev).astype(jnp.int32)
        window = jnp.zeros((src_count * rows_dev, feat_width), segment.dtype)
        window = lax.dynamic_update_slice_in_dim(window, segment, shift_rows, 0)
        window = window.reshape(src_count, row_tiles, tile_size, feat_width)

        def visit(visit_idx, summed):
            source = first_src + visit_idx
            valid_src = (source < blocks).astype(jnp.float32)
            src_clamp = jnp.minimum(source, blocks - 1)
            col_marks = lax.dynamic_index_in_dim(col_marks_all, src_clamp, 0, keepdims=False)
            tile_vals = lax.dynamic_index_in_dim(tile_values, src_clamp, 0, keepdims=False)
            row_marks = lax.dynamic_index_in_dim(row_marks_all, src_clamp, 0, keepdims=False)
            src_block = lax.dynamic_index_in_dim(window, visit_idx, 0, keepdims=False)
            picked = jnp.einsum(
                "kc,cjh->kjh", col_marks, src_block, preferred_element_type=jnp.float32
            ).astype(jnp.bfloat16)
            products = jnp.einsum(
                "kij,kjh->kih", tile_vals, picked, preferred_element_type=jnp.float32
            )
            placed = jnp.einsum("kr,kih->rih", row_marks, products)
            return summed + valid_src * placed.reshape(rows_dev, feat_width)

        return lax.fori_loop(0, src_count, visit, running)

    empty = jnp.zeros((rows_dev, feat_width), jnp.float32)
    gathered = absorb(
        empty,
        jax.tree.map(lambda a: lax.all_gather(a, "blk", axis=0, tiled=True), node_feats),
        jnp.int32(0),
    )
    combined = ((1.0 + eps_self[0]) * node_feats.astype(jnp.float32) + gathered).astype(
        jnp.bfloat16
    )
    quarter = lax.all_to_all(combined, "feat", split_axis=0, concat_axis=1, tiled=True)
    first_full, first_bias, second_full, second_bias = (
        lax.all_gather(w_one, "feat", axis=1, tiled=True),
        lax.all_gather(b_one, "feat", axis=0, tiled=True),
        lax.all_gather(w_two, "feat", axis=0, tiled=True),
        lax.all_gather(b_two, "feat", axis=0, tiled=True),
    )
    pre = jnp.dot(quarter, first_full, preferred_element_type=jnp.float32) + first_bias.astype(
        jnp.float32
    )
    hidden = jnp.maximum(pre, 0.0).astype(jnp.bfloat16)
    out_rows = (
        jnp.dot(hidden, second_full, preferred_element_type=jnp.float32)
        + second_bias.astype(jnp.float32)
    ).astype(jnp.bfloat16)
    return lax.all_to_all(out_rows, "feat", split_axis=1, concat_axis=0, tiled=True)


def solution(mesh):
    placed = (
        P("blk", "feat"),
        P("blk", None),
        P("blk", None),
        P("blk", None, None, None),
        P(),
        P(None, "feat"),
        P("feat"),
        P("feat", None),
        P("feat"),
    )
    return jax.shard_map(
        on_device, mesh=mesh, in_specs=placed, out_specs=P("blk", "feat"), check_vma=False
    )
```

profile of v0, /device:TPU:1, one launch (start us, length us, event | category | flops | bytes accessed | tf_op | source)
XLA Modules:
  0.0 283.9 jit_solution(17830095851559013923)
XLA Ops:
  6.5 0.0 all-gather.2.cloned.1.call-start
  6.5 0.7 all-gather.2.cloned.1.call-update
  7.9 0.8 fusion.20
  8.7 125.7 %all-gather.2.cloned.1.call-done = bf16[65536,64]{0,1:T(8,128)(2,1)} async-done(((bf16[8192,64]{0,1:T(8,128)(2,1)}), bf16[65536,64]{0,1:T(8,128)(2,1)}) %all-gather.2.cloned.1.call-update) | async-done | bytes 8388624 | tf_op jit(solution)/shard_map/all_gather | solution.py:51
  134.4 8.9 %copy.32 = bf16[8,8,512,128]{3,2,1,0:T(8,128)(2,1)} copy(bf16[8,8,512,128]{3,1,2,0:T(8,128)(2,1)} %bitcast.56) | data formatting | bytes 16777216
  143.3 0.0 copy-start
  143.3 82.2 %while.15 = (s32[]{:T(128)}, f32[8192,64]{0,1:T(8,128)S(1)}, bf16[8,128,64]{1,2,0:T(8,128)(2,1)S(1)}, bf16[8,128,128,128]{3,2,1,0:T(8,128)(2,1)}, bf16[8,128,64]...) while((s32[]{:T(128)}, f32[8192,64]{0,1:T(8,128)S(1)}, ...), condition=%wide.region_1.2_spmd.clone, body=%wide.region_0.1_spmd.clone.sunk | while | flops 538968064 | bytes 22053044 | solution.py:46
  143.3 2.0 convolution_convert_fusion.2
  145.4 5.2 %fusion.40 = bf16[128,128,64]{1,2,0:T(8,128)(2,1)S(1)} fusion(bf16[8,128,128,128]{3,2,1,0:T(8,128)(2,1)} %get-tuple-element.257, s32[]{:T(128)S(6)} %select_n.28, bf16[128,128,64]{1,0,2:T(8,128)(2,1)S(1)} %convolution_convert_fusion.2), kind=kOutput, calls=%fused_computation.clone.1 | convolution fusion | flops 268435456 | bytes 8388612 | tf_op jit(solution)/shard_map/while/body/eval_jaxpr/kij,kjh->kih/dot_general | solution.py:40
  150.6 1.5 fusion.41
  152.0 1.6 bitcast_add_fusion.2
  153.7 2.0 convolution_convert_fusion.2
  155.7 5.2 %fusion.40 = bf16[128,128,64]{1,2,0:T(8,128)(2,1)S(1)} fusion(bf16[8,128,128,128]{3,2,1,0:T(8,128)(2,1)} %get-tuple-element.257, s32[]{:T(128)S(6)} %select_n.28, bf16[128,128,64]{1,0,2:T(8,128)(2,1)S(1)} %convolution_convert_fusion.2), kind=kOutput, calls=%fused_computation.clone.1 | convolution fusion | flops 268435456 | bytes 8388612 | tf_op jit(solution)/shard_map/while/body/eval_jaxpr/kij,kjh->kih/dot_general | solution.py:40
  160.8 1.5 fusion.41
  162.3 1.6 bitcast_add_fusion.2
  164.0 2.0 convolution_convert_fusion.2
  165.9 5.2 %fusion.40 = bf16[128,128,64]{1,2,0:T(8,128)(2,1)S(1)} fusion(bf16[8,128,128,128]{3,2,1,0:T(8,128)(2,1)} %get-tuple-element.257, s32[]{:T(128)S(6)} %select_n.28, bf16[128,128,64]{1,0,2:T(8,128)(2,1)S(1)} %convolution_convert_fusion.2), kind=kOutput, calls=%fused_computation.clone.1 | convolution fusion | flops 268435456 | bytes 8388612 | tf_op jit(solution)/shard_map/while/body/eval_jaxpr/kij,kjh->kih/dot_general | solution.py:40
  171.1 1.5 fusion.41
  172.6 1.6 bitcast_add_fusion.2
  174.2 2.0 convolution_convert_fusion.2
  176.2 5.2 %fusion.40 = bf16[128,128,64]{1,2,0:T(8,128)(2,1)S(1)} fusion(bf16[8,128,128,128]{3,2,1,0:T(8,128)(2,1)} %get-tuple-element.257, s32[]{:T(128)S(6)} %select_n.28, bf16[128,128,64]{1,0,2:T(8,128)(2,1)S(1)} %convolution_convert_fusion.2), kind=kOutput, calls=%fused_computation.clone.1 | convolution fusion | flops 268435456 | bytes 8388612 | tf_op jit(solution)/shard_map/while/body/eval_jaxpr/kij,kjh->kih/dot_general | solution.py:40
  181.4 1.5 fusion.41
  182.8 1.6 bitcast_add_fusion.2
  184.5 2.0 convolution_convert_fusion.2
  186.5 5.2 %fusion.40 = bf16[128,128,64]{1,2,0:T(8,128)(2,1)S(1)} fusion(bf16[8,128,128,128]{3,2,1,0:T(8,128)(2,1)} %get-tuple-element.257, s32[]{:T(128)S(6)} %select_n.28, bf16[128,128,64]{1,0,2:T(8,128)(2,1)S(1)} %convolution_convert_fusion.2), kind=kOutput, calls=%fused_computation.clone.1 | convolution fusion | flops 268435456 | bytes 8388612 | tf_op jit(solution)/shard_map/while/body/eval_jaxpr/kij,kjh->kih/dot_general | solution.py:40
  191.7 1.5 fusion.41
  193.1 1.6 bitcast_add_fusion.2
  194.8 2.0 convolution_convert_fusion.2
  196.8 5.2 %fusion.40 = bf16[128,128,64]{1,2,0:T(8,128)(2,1)S(1)} fusion(bf16[8,128,128,128]{3,2,1,0:T(8,128)(2,1)} %get-tuple-element.257, s32[]{:T(128)S(6)} %select_n.28, bf16[128,128,64]{1,0,2:T(8,128)(2,1)S(1)} %convolution_convert_fusion.2), kind=kOutput, calls=%fused_computation.clone.1 | convolution fusion | flops 268435456 | bytes 8388612 | tf_op jit(solution)/shard_map/while/body/eval_jaxpr/kij,kjh->kih/dot_general | solution.py:40
  201.9 1.5 fusion.41
  203.4 1.6 bitcast_add_fusion.2
  205.1 2.0 convolution_convert_fusion.2
  207.0 5.2 %fusion.40 = bf16[128,128,64]{1,2,0:T(8,128)(2,1)S(1)} fusion(bf16[8,128,128,128]{3,2,1,0:T(8,128)(2,1)} %get-tuple-element.257, s32[]{:T(128)S(6)} %select_n.28, bf16[128,128,64]{1,0,2:T(8,128)(2,1)S(1)} %convolution_convert_fusion.2), kind=kOutput, calls=%fused_computation.clone.1 | convolution fusion | flops 268435456 | bytes 8388612 | tf_op jit(solution)/shard_map/while/body/eval_jaxpr/kij,kjh->kih/dot_general | solution.py:40
  212.2 1.5 fusion.41
  213.7 1.6 bitcast_add_fusion.2
  215.3 2.0 convolution_convert_fusion.2
  217.3 5.2 %fusion.40 = bf16[128,128,64]{1,2,0:T(8,128)(2,1)S(1)} fusion(bf16[8,128,128,128]{3,2,1,0:T(8,128)(2,1)} %get-tuple-element.257, s32[]{:T(128)S(6)} %select_n.28, bf16[128,128,64]{1,0,2:T(8,128)(2,1)S(1)} %convolution_convert_fusion.2), kind=kOutput, calls=%fused_computation.clone.1 | convolution fusion | flops 268435456 | bytes 8388612 | tf_op jit(solution)/shard_map/while/body/eval_jaxpr/kij,kjh->kih/dot_general | solution.py:40
  222.5 1.5 fusion.41
  223.9 1.6 bitcast_add_fusion.2
  225.6 0.0 copy-done
  225.6 0.2 add_convert_fusion
  225.9 0.0 copy-start.5
  225.9 0.0 copy-start.3
  225.9 0.0 copy-start.4
  225.9 0.0 copy-start.1
  225.9 0.0 copy-start.2
  225.9 1.0 copy.39
  227.0 5.3 %all-to-all-start = ((bf16[4,2048,64]{1,2,0:T(8,128)(2,1)}), bf16[4,2048,64]{1,2,0:T(8,128)(2,1)S(1)}, u32[]{:S(2)}, u32[]{:S(2)}) async-start(bf16[4,2048,64]{1,2,0:T(8,128)(2,1)} %bitcast.41), calls=%async_computation | async-start | bytes 2097152 | tf_op jit(solution)/shard_map/all_to_all | solution.py:57
  232.2 0.0 copy-done.5
  232.2 0.6 dynamic-slice
  233.5 0.0 copy-done.3
  233.5 0.2 dynamic-update-slice.1
  233.8 0.0 copy-done.4
  233.8 0.2 dynamic-update-slice
  234.0 13.1 %all-reduce.2 = (bf16[256]{0:T(256)(128)(2,1)S(1)}, bf16[256]{0:T(256)(128)(2,1)S(1)}) all-reduce(bf16[256]{0:T(256)(128)(2,1)S(1)} %dynamic-update-slice.1, bf16[256]{0:T(256)(128)(2,1)S(1)} %dynamic-update-slice), channel_id=1, replica_groups=mesh['blk'=8,'feat'=4] {'feat'}, use_global_device_ids=true, to_apply=%add.1 | all-reduce | flops 512 | bytes 2048
  247.1 0.0 copy-done.1
  247.1 6.3 %all_gather.16 = bf16[256,256]{0,1:T(8,128)(2,1)S(1)} all-gather(bf16[256,64]{0,1:T(8,128)(2,1)S(1)} %copy-done.1), channel_id=1, replica_groups=mesh['blk'=8,'feat'=4] {'feat'}, dimensions={1}, use_global_device_ids=true | all-gather | bytes 163840 | tf_op jit(solution)/shard_map/all_gather | solution.py:59
  253.4 0.0 copy-done.2
  253.4 5.4 %all_gather.18 = bf16[256,256]{1,0:T(8,128)(2,1)S(1)} all-gather(bf16[64,256]{1,0:T(8,128)(2,1)S(1)} %copy-done.2), channel_id=1, replica_groups=mesh['blk'=8,'feat'=4] {'feat'}, dimensions={0}, use_global_device_ids=true | all-gather | bytes 163840 | tf_op jit(solution)/shard_map/all_gather | solution.py:61
  258.8 0.0 all-to-all-done
  258.8 0.9 fusion.17
  259.7 16.3 %all_to_all.38 = bf16[2048,4,64]{0,2,1:T(8,128)(2,1)S(1)} all-to-all(bf16[2048,4,64]{0,2,1:T(8,128)(2,1)S(1)} %bitcast.60), channel_id=1, replica_groups=mesh['blk'=8,'feat'=4] {'feat'}, dimensions={1} | all-to-all | bytes 2097152 | tf_op jit(solution)/shard_map/all_to_all | solution.py:72
  276.0 1.0 copy.31
  (5 shorter events, 0.0 us)
Async XLA Ops:
  6.5 127.9 %all-gather.2.cloned.1.call-start = ((), (), s32[]{:S(2)}) async-start(), calls=%async_computation.2 | async-start | bytes 9437184 | tf_op jit(solution)/shard_map/all_gather | solution.py:51
  143.3 82.3 %copy-start = (bf16[8192,64]{0,1:T(8,128)(2,1)S(1)}, bf16[8192,64]{0,1:T(8,128)(2,1)}, u32[]{:S(2)}) copy-start(bf16[8192,64]{0,1:T(8,128)(2,1)} %param.11) | copy-start | bytes 3145732
  225.9 6.4 %copy-start.5 = (u32[32]{0:T(128)S(1)}, u32[32]{0:T(128)}, u32[]{:S(2)}) copy-start(u32[32]{0:T(128)} %constant.80) | copy-start | bytes 388
  225.9 7.7 %copy-start.3 = (bf16[64]{0:T(256)(128)(2,1)S(1)}, bf16[64]{0:T(256)(128)(2,1)}, u32[]{:S(2)}) copy-start(bf16[64]{0:T(256)(128)(2,1)} %param.19) | copy-start | bytes 388
  225.9 7.9 %copy-start.4 = (bf16[64]{0:T(256)(128)(2,1)S(1)}, bf16[64]{0:T(256)(128)(2,1)}, u32[]{:S(2)}) copy-start(bf16[64]{0:T(256)(128)(2,1)} %param.17) | copy-start | bytes 388
  225.9 21.2 %copy-start.1 = (bf16[256,64]{0,1:T(8,128)(2,1)S(1)}, bf16[256,64]{0,1:T(8,128)(2,1)}, u32[]{:S(2)}) copy-start(bf16[256,64]{0,1:T(8,128)(2,1)} %param.16) | copy-start | bytes 98308
  225.9 27.5 %copy-start.2 = (bf16[64,256]{1,0:T(8,128)(2,1)S(1)}, bf16[64,256]{1,0:T(8,128)(2,1)}, u32[]{:S(2)}) copy-start(bf16[64,256]{1,0:T(8,128)(2,1)} %param.18) | copy-start | bytes 98308
  227.0 31.9 %all-to-all-start = ((bf16[4,2048,64]{1,2,0:T(8,128)(2,1)}), bf16[4,2048,64]{1,2,0:T(8,128)(2,1)S(1)}, u32[]{:S(2)}, u32[]{:S(2)}) async-start(bf16[4,2048,64]{1,2,0:T(8,128)(2,1)} %bitcast.41), calls=%async_computation | async-start | bytes 2097152 | tf_op jit(solution)/shard_map/all_to_all | solution.py:57
Sparse Core Ops, SparseCore 0:
  9.5 124.8 all-gather.1
where the time goes:
time: 286 us; the launch traced here: 284 us
  waiting for transfers between devices  126 us (44%)
  matrix products  69.8 us (24%)
  blocking collectives  41 us (14%)
  between operations  14.8 us (5%)
  other arithmetic  14.1 us (5%)
  local copies, waits for them, and re-layouts  12.2 us (4%)
  starting transfers between devices  5.27 us (2%)
    all_gather x1, waiting for transfers between devices, on_device(): lax.all_gather(a, 'blk', axis=0, tiled=True)  126 us
    dot_general x8, matrix products, visit(): jnp.einsum('kij,kjh->kih', tile_vals, picked, preferred_element_type=jnp....  41.4 us
    all_to_all x1, blocking collectives, on_device(): lax.all_to_all(out_rows, 'feat', split_axis=1, concat_axis=0, tiled=True)  16.3 us
    dot_general x8, matrix products, visit(): jnp.einsum('kc,cjh->kjh', col_marks, src_block, preferred_element_type=jn...  15.8 us
    unnamed x1, blocking collectives  13.1 us
    add x8, other arithmetic, visit(): return summed + valid_src * placed.reshape(rows_dev, feat_width)  13 us
    dot_general x8, matrix products, visit(): placed = jnp.einsum('kr,kih->rih', row_marks, products)  11.7 us
    unnamed x18, local copies, waits for them, and re-layouts  10.1 us
  transfers between devices with their start and end apart: 2, of which 1 were waited for; matrix products, arithmetic and copies ran while one was open for 1% of the time, Pallas kernels for 0%

commit v1 on v0

v1 whole, which is shorter than its diff:
```python
import functools

import jax
import jax.numpy as jnp
from jax import lax
from jax.experimental import pallas as pl
from jax.experimental.pallas import tpu as pltpu
from jax.sharding import PartitionSpec as P

MESH = pl.DeviceIdType.MESH
CHUNKS = 4
PIECES = 4
VMEM_LIMIT = 60 * 1024 * 1024


def gather_kernel(lines, n_feat, x_ref, w_ref, all_ref, wall_ref, send_sems, recv_sems, w_send, w_recv, own_sems):
    blk, feat = lax.axis_index("blk"), lax.axis_index("feat")
    line, side = lax.div(blk, 2), lax.rem(blk, 2)
    partner = line * 2 + (1 - side)
    mate = line + 1 - 2 * lax.rem(line, 2)
    mate_block = mate * 2 + side
    has_low, has_high = line > 0, line < lines - 1
    low, high = blk - 2, blk + 2
    depth = x_ref.shape[0] // CHUNKS
    half = CHUNKS // 2
    w_rows = w_ref.shape[0]

    barrier = pltpu.get_barrier_semaphore()
    pl.semaphore_signal(barrier, inc=1, device_id={"blk": partner}, device_id_type=MESH)
    for k in range(1, n_feat):
        pl.semaphore_signal(barrier, inc=1, device_id={"feat": lax.rem(feat + k, n_feat)}, device_id_type=MESH)

    @pl.when(has_low)
    def _():
        pl.semaphore_signal(barrier, inc=1, device_id={"blk": low}, device_id_type=MESH)

    @pl.when(has_high)
    def _():
        pl.semaphore_signal(barrier, inc=1, device_id={"blk": high}, device_id_type=MESH)

    pl.semaphore_wait(barrier, n_feat + has_low.astype(jnp.int32) + has_high.astype(jnp.int32))

    def piece(b, c):
        return all_ref.at[b, pl.ds(c * depth, depth), :]

    def copy(way, target, b, c, own=False):
        source = x_ref.at[pl.ds(c * depth, depth), :] if own else piece(b, c)
        return pltpu.make_async_remote_copy(
            src_ref=source,
            dst_ref=piece(b, c),
            send_sem=send_sems.at[way, b, c],
            recv_sem=recv_sems.at[b, c],
            device_id={"blk": target},
            device_id_type=MESH,
        )

    def arrive(b, c):
        copy(2, partner, b, c).wait_recv()

    def weight_copy(k):
        return pltpu.make_async_remote_copy(
            src_ref=w_ref,
            dst_ref=wall_ref.at[pl.ds(feat * w_rows, w_rows), :],
            send_sem=w_send.at[k - 1],
            recv_sem=w_recv.at[k - 1],
            device_id={"feat": lax.rem(feat + k, n_feat)},
            device_id_type=MESH,
        )

    def weight_arrive(k):
        rows = pl.ds(lax.rem(feat + n_feat - k, n_feat) * w_rows, w_rows)
        pltpu.make_async_remote_copy(
            src_ref=w_ref,
            dst_ref=wall_ref.at[rows, :],
            send_sem=w_send.at[k - 1],
            recv_sem=w_recv.at[k - 1],
            device_id={"feat": lax.rem(feat + k, n_feat)},
            device_id_type=MESH,
        ).wait_recv()

    def sends(act, c, b, lower_ok, upper_ok, across_ok, own=False):
        if lower_ok is not None:
            @pl.when(lower_ok)
            def _():
                act(copy(0, low, b, c, own))
        if upper_ok is not None:
            @pl.when(upper_ok)
            def _():
                act(copy(1, high, b, c, own))
        if across_ok is True:
            act(copy(2, partner, b, c, own))
        else:
            @pl.when(across_ok)
            def _():
                act(copy(2, partner, b, c, own))

    def extra(act, c):
        @pl.when(mate > line)
        def _():
            act(copy(1, high, partner, c))

        @pl.when(mate < line)
        def _():
            act(copy(0, low, partner, c))

    def plan(act, wait):
        for c in range(CHUNKS):
            sends(act, c, blk, has_low, has_high, True, own=True)
        for step in range(1, lines):
            for c in range(CHUNKS):
                for above in (True, False):
                    spot = line + step if above else line - step
                    b = spot * 2 + side

                    @pl.when(spot < lines if above else spot >= 0)
                    def _(b=b, above=above, c=c):
                        if wait:
                            arrive(b, c)
                        across = True if c >= half else b != mate_block
                        sends(act, c, b, has_low if above else None, None if above else has_high, across)
            if step == 1:
                for c in range(half):
                    if wait:
                        arrive(partner, c)
                    extra(act, c)

    own_copies = [
        pltpu.make_async_copy(x_ref, all_ref.at[blk], own_sems.at[0]),
        pltpu.make_async_copy(w_ref, wall_ref.at[pl.ds(feat * w_rows, w_rows), :], own_sems.at[1]),
    ]
    for own in own_copies:
        own.start()
    for k in range(1, n_feat):
        weight_copy(k).start()
    plan(lambda d: d.start(), True)
    for c in range(half, CHUNKS):
        arrive(partner, c)
    for step in range(1, lines):
        spot = lax.rem(line + step, lines)
        for c in range(CHUNKS):
            arrive(spot * 2 + (1 - side), c)
    for k in range(1, n_feat):
        weight_arrive(k)
    plan(lambda d: d.wait_send(), False)
    for k in range(1, n_feat):
        weight_copy(k).wait_send()
    for own in own_copies:
        own.wait()


def gather_all(lines, n_feat, x_t, w_pack):
    feats, rows = x_t.shape
    blocks = lines * 2
    return pl.pallas_call(
        functools.partial(gather_kernel, lines, n_feat),
        out_shape=(
            jax.ShapeDtypeStruct((blocks, feats, rows), x_t.dtype),
            jax.ShapeDtypeStruct((n_feat * w_pack.shape[0], w_pack.shape[1]), w_pack.dtype),
        ),
        in_specs=[pl.BlockSpec(memory_space=pltpu.VMEM)] * 2,
        out_specs=(pl.BlockSpec(memory_space=pl.ANY), pl.BlockSpec(memory_space=pltpu.VMEM)),
        scratch_shapes=[
            pltpu.SemaphoreType.DMA((3, blocks, CHUNKS)),
            pltpu.SemaphoreType.DMA((blocks, CHUNKS)),
            pltpu.SemaphoreType.DMA((n_feat - 1,)),
            pltpu.SemaphoreType.DMA((n_feat - 1,)),
            pltpu.SemaphoreType.DMA((2,)),
        ],
        compiler_params=pltpu.CompilerParams(
            collective_id=0, has_side_effects=True, vmem_limit_bytes=VMEM_LIMIT
        ),
    )(x_t, w_pack)


def aggregate_kernel(group, rows_ref, cols_ref, eps_ref, x_ref, tiles_ref, own_ref, out_ref, acc):
    src = pl.program_id(0)
    slots, tile = tiles_ref.shape[1], tiles_ref.shape[2]

    @pl.when(src == 0)
    def _():
        acc[...] = jnp.zeros_like(acc)

    @pl.loop(0, slots // group)
    def _(g):
        products = []
        for i in range(group):
            k = g * group + i
            lanes = pl.ds(pl.multiple_of(cols_ref[src, k] * tile, tile), tile)
            products.append(
                lax.dot_general(
                    x_ref[0, :, lanes], tiles_ref[0, k], (((1,), (1,)), ((), ())),
                    preferred_element_type=jnp.float32,
                )
            )
        for i in range(group):
            r = rows_ref[src, g * group + i]
            acc[r] = acc[r] + products[i]

    @pl.when(src == pl.num_programs(0) - 1)
    def _():
        scale = 1.0 + eps_ref[0]
        for r in range(acc.shape[0]):
            lanes = pl.ds(r * tile, tile)
            own = own_ref[:, lanes].astype(jnp.float32)
            out_ref[:, lanes] = (scale * own + acc[r]).astype(out_ref.dtype)


def aggregate(x_all, tile_rows, tile_cols, tile_values, eps_self, x_t):
    blocks, slots, tile, _ = tile_values.shape
    feats, rows = x_t.shape
    group = 8 if slots % 8 == 0 else 1
    return pl.pallas_call(
        functools.partial(aggregate_kernel, group),
        out_shape=jax.ShapeDtypeStruct((feats, rows), x_t.dtype),
        grid_spec=pltpu.PrefetchScalarGridSpec(
            num_scalar_prefetch=3,
            grid=(blocks,),
            in_specs=[
                pl.BlockSpec((1, feats, rows), lambda s, *_: (s, 0, 0)),
                pl.BlockSpec((1, slots, tile, tile), lambda s, *_: (s, 0, 0, 0)),
                pl.BlockSpec((feats, rows), lambda s, *_: (0, 0)),
            ],
            out_specs=pl.BlockSpec((feats, rows), lambda s, *_: (0, 0)),
            scratch_shapes=[pltpu.VMEM((rows // tile, feats, tile), jnp.float32)],
        ),
        compiler_params=pltpu.CompilerParams(vmem_limit_bytes=VMEM_LIMIT),
    )(tile_rows, tile_cols, eps_self, x_all, tile_values, x_t)


def perceptron_kernel(n_feat, comb_ref, w_ref, out_ref, rows_in, staged, in_send, in_recv, out_send, out_recv, own_sems):
    feat = lax.axis_index("feat")
    feats = comb_ref.shape[0]
    share = rows_in.shape[1]
    width = share // PIECES
    full = rows_in.shape[0]

    barrier = pltpu.get_barrier_semaphore()
    for k in range(1, n_feat):
        pl.semaphore_signal(barrier, inc=1, device_id={"feat": lax.rem(feat + k, n_feat)}, device_id_type=MESH)
    pl.semaphore_wait(barrier, n_feat - 1)

    def lanes_of(owner, c):
        return pl.ds(pl.multiple_of(owner * share + c * width, width), width)

    def rows_of(owner):
        return pl.ds(pl.multiple_of(owner * feats, feats), feats)

    def inward(k, c, receive=False):
        peer = lax.rem(feat + k, n_feat)
        writer = lax.rem(feat + n_feat - k, n_feat) if receive else feat
        return pltpu.make_async_remote_copy(
            src_ref=comb_ref.at[:, lanes_of(peer, c)],
            dst_ref=rows_in.at[rows_of(writer), pl.ds(c * width, width)],
            send_sem=in_send.at[k - 1, c],
            recv_sem=in_recv.at[k - 1, c],
            device_id={"feat": peer},
            device_id_type=MESH,
        )

    def outward(k, c, receive=False):
        peer = lax.rem(feat + k, n_feat)
        writer = lax.rem(feat + n_feat - k, n_feat) if receive else feat
        return pltpu.make_async_remote_copy(
            src_ref=staged.at[rows_of(peer), pl.ds(c * width, width)],
            dst_ref=out_ref.at[:, lanes_of(writer, c)],
            send_sem=out_send.at[k - 1, c],
            recv_sem=out_recv.at[k - 1, c],
            device_id={"feat": peer},
            device_id_type=MESH,
        )

    def own_in(c):
        return pltpu.make_async_copy(
            comb_ref.at[:, lanes_of(feat, c)], rows_in.at[rows_of(feat), pl.ds(c * width, width)], own_sems.at[0, c]
        )

    def own_out(c):
        return pltpu.make_async_copy(
            staged.at[rows_of(feat), pl.ds(c * width, width)], out_ref.at[:, lanes_of(feat, c)], own_sems.at[1, c]
        )

    for c in range(PIECES):
        for k in range(1, n_feat):
            inward(k, c).start()
        own_in(c).start()
    first = w_ref[:, :full]
    second = w_ref[:, full : 2 * full]
    bias_one = w_ref[:, 2 * full : 2 * full + 1].astype(jnp.float32)
    bias_two = w_ref[:, 2 * full + 1 : 2 * full + 2].astype(jnp.float32)
    for c in range(PIECES):
        own_in(c).wait()
        for k in range(1, n_feat):
            inward(k, c, True).wait_recv()
        at = pl.ds(c * width, width)
        pre = jnp.dot(first, rows_in[:, at], preferred_element_type=jnp.float32) + bias_one
        hidden = jnp.maximum(pre, 0.0).astype(jnp.bfloat16)
        out = lax.dot_general(second, hidden, (((0,), (0,)), ((), ())), preferred_element_type=jnp.float32)
        staged[:, at] = (out + bias_two).astype(staged.dtype)
        for k in range(1, n_feat):
            outward(k, c).start()
        own_out(c).start()
    for c in range(PIECES):
        for k in range(1, n_feat):
            outward(k, c, True).wait_recv()
        own_out(c).wait()
        for k in range(1, n_feat):
            inward(k, c).wait_send()
            outward(k, c).wait_send()


def perceptron(n_feat, comb_t, w_all):
    feats, rows = comb_t.shape
    share = rows // n_feat
    pair_sems = pltpu.SemaphoreType.DMA((n_feat - 1, PIECES))
    return pl.pallas_call(
        functools.partial(perceptron_kernel, n_feat),
        out_shape=jax.ShapeDtypeStruct((feats, rows), comb_t.dtype),
        in_specs=[pl.BlockSpec(memory_space=pltpu.VMEM)] * 2,
        out_specs=pl.BlockSpec(memory_space=pltpu.VMEM),
        scratch_shapes=[
            pltpu.VMEM((n_feat * feats, share), comb_t.dtype),
            pltpu.VMEM((n_feat * feats, share), comb_t.dtype),
            pair_sems, pair_sems, pair_sems, pair_sems,
            pltpu.SemaphoreType.DMA((2, PIECES)),
        ],
        compiler_params=pltpu.CompilerParams(
            collective_id=1, has_side_effects=True, vmem_limit_bytes=VMEM_LIMIT
        ),
    )(comb_t, w_all)


def solution(mesh):
    lines, n_feat = mesh.shape["blk"] // 2, mesh.shape["feat"]

    def on_device(node_feats, tile_rows, tile_cols, tile_values, eps_self, w_one, b_one, w_two, b_two):
        x_t = node_feats.T
        biases = jnp.stack([b_one, b_two], axis=1)
        biases = jnp.pad(biases, ((0, 0), (0, tile_values.shape[2] - 2)))
        w_pack = jnp.concatenate([w_one.T, w_two, biases], axis=1)
        x_all, w_all = gather_all(lines, n_feat, x_t, w_pack)
        comb_t = aggregate(x_all, tile_rows, tile_cols, tile_values, eps_self, x_t)
        return perceptron(n_feat, comb_t, w_all).T

    return jax.shard_map(
        on_device,
        mesh=mesh,
        in_specs=(
            P("blk", "feat"),
            P("blk", None),
            P("blk", None),
            P("blk", None, None, None),
            P(),
            P(None, "feat"),
            P("feat"),
            P("feat", None),
            P("feat"),
        ),
        out_specs=P("blk", "feat"),
        check_vma=False,
    )
```

time: 286 us -> 171 us (0.60)
  Pallas kernels: 0 us -> 165 us
  waiting for transfers between devices: 126 us -> 0 us
  matrix products: 69.8 us -> 0 us
  blocking collectives: 41 us -> 0 us
  between operations: 14.8 us -> 0.67 us
  other arithmetic: 14.1 us -> 2.1 us
  local copies, waits for them, and re-layouts: 12.2 us -> 2.38 us
  starting transfers between devices: 5.27 us -> 0 us
    pallas_call x0 -> x3, Pallas kernels: none -> 165 us  [the longest x1 93.8 us: gather_all(): pl.pallas_call(functools.partial(gather_kernel, lines, n_feat), out_shape...]
    all_gather x1 -> x0, waiting for transfers between devices: 126 us -> none  [on_device(): lax.all_gather(a, 'blk', axis=0, tiled=True)]
    dot_general x25 -> x0, matrix products: 69.8 us -> none  [the longest x8 41.4 us: visit(): jnp.einsum('kij,kjh->kih', tile_vals, picked, preferred_element_type=jnp....]
    all_to_all x1 -> x0, blocking collectives: 16.3 us -> none  [on_device(): lax.all_to_all(out_rows, 'feat', split_axis=1, concat_axis=0, tiled=True)]
    unnamed x1 -> x0, blocking collectives: 13.1 us -> none
    add x8 -> x0, other arithmetic: 13 us -> none  [visit(): return summed + valid_src * placed.reshape(rows_dev, feat_width)]
    all_gather x2 -> x0, blocking collectives: 11.7 us -> none  [the longest x1 6.29 us: on_device(): lax.all_gather(w_one, 'feat', axis=1, tiled=True)]
    unnamed x18 -> x1, local copies, waits for them, and re-layouts: 10.1 us -> 2.26 us
  transfers between devices with their start and end apart: 2 -> 0, of which waited for: 1 -> 0; matrix products, arithmetic and copies ran while one was open for 1% -> 0% of each run, Pallas kernels for 0% -> 0%
where the time goes in v1:
time: 171 us; the launch traced here: 170 us
  Pallas kernels  165 us (96%)
  local copies, waits for them, and re-layouts  2.38 us (1%)
  other arithmetic  2.1 us (1%)
    pallas_call x1, Pallas kernels, gather_all(): pl.pallas_call(functools.partial(gather_kernel, lines, n_feat), out_shape...  93.8 us
    pallas_call x1, Pallas kernels, aggregate(): pl.pallas_call(functools.partial(aggregate_kernel, group), out_shape=jax....  42.1 us
    pallas_call x1, Pallas kernels, perceptron(): pl.pallas_call(functools.partial(perceptron_kernel, n_feat), out_shape=ja...  29.2 us

profile of v1, /device:TPU:1, one launch (start us, length us, event | category | flops | bytes accessed | tf_op | source)
XLA Modules:
  0.0 170.2 jit_solution(2921686363038055960)
XLA Ops:
  0.7 0.7 pad_maximum_fusion
  1.3 0.1 copy.12
  1.4 1.4 fusion.1.w_ref
  2.9 93.8 %shard_map.91 = (bf16[8,64,8192]{2,1,0:T(8,128)(2,1)}, bf16[256,640]{1,0:T(8,128)(2,1)}) custom-call(bf16[64,8192]{1,0:T(8,128)(2,1)} %bitcast.5, bf16[64,640]{1,0:T(8,128)(2,1)} %fusion.1.w_ref), custom_call_target="tpu_custom_call" | custom-call | tf_op jit(solution)/shard_map/pallas_call | solution.py:154
  96.7 42.1 %shard_map.92.comb_ref = bf16[64,8192]{1,0:T(8,128)(2,1)} custom-call(s32[8,128]{1,0:T(8,128)} %rows_ref.1, s32[8,128]{1,0:T(8,128)} %cols_ref.1, f32[1]{0:T(128)S(6)} %copy.14.eps_ref, bf16[8,64,8192]{2,1,0:T(8,128)(2,1)} %get-tuple-element.7.x_ref, bf16[8,128,128,128]{3,2,1,0:T(8,128)(2,1)} %tiles_ref.1, bf16[64,8192]{1,0:T(8,128)(2,1)} %bitcast.6), custom_call_target="tpu_custom_call" | custom-call | tf_op jit(solution)/shard_map/pallas_call | solution.py:212
  138.8 29.2 %shard_map.93 = bf16[64,8192]{1,0:T(8,128)(2,1)} custom-call(bf16[64,8192]{1,0:T(8,128)(2,1)} %shard_map.92.comb_ref, bf16[256,640]{1,0:T(8,128)(2,1)} %get-tuple-element.8.w_ref), custom_call_target="tpu_custom_call" | custom-call | tf_op jit(solution)/shard_map/pallas_call | solution.py:315
  168.0 2.3 %copy.15 = bf16[8192,64]{0,1:T(8,128)(2,1)} copy(bf16[8192,64]{0,1:T(8,128)(2,1)} %bitcast.7) | data formatting | bytes 2097152

commit v2 on v1

--- a/solution.py
+++ b/solution.py
@@ -10,10 +10,16 @@
 MESH = pl.DeviceIdType.MESH
 CHUNKS = 4
 PIECES = 4
+PARTS = 4
+DEEP = 6
+GROUP = 8
 VMEM_LIMIT = 60 * 1024 * 1024
 
 
-def gather_kernel(lines, n_feat, x_ref, w_ref, all_ref, wall_ref, send_sems, recv_sems, w_send, w_recv, own_sems):
+def gather_kernel(
+    lines, n_feat, x_ref, w_ref, meta_ref, eps_ref, tiles_ref, comb_ref, wall_ref,
+    all_ref, along, across_buf, tile_buf, sums, send_sems, recv_sems, w_send, w_recv, own_sems, tile_sems,
+):
     blk, feat = lax.axis_index("blk"), lax.axis_index("feat")
     line, side = lax.div(blk, 2), lax.rem(blk, 2)
     partner = line * 2 + (1 - side)
@@ -103,128 +109,177 @@
         def _():
             act(copy(0, low, partner, c))
 
-    def plan(act, wait):
+    def relay(act, wait, step, c):
+        for above in (True, False):
+            spot = line + step if above else line - step
+            b = spot * 2 + side
+
+            @pl.when(spot < lines if above else spot >= 0)
+            def _(b=b, above=above):
+                if wait:
+                    arrive(b, c)
+                across = True if c >= half else b != mate_block
+                sends(act, c, b, has_low if above else None, None if above else has_high, across)
+
+    slots, tile = tiles_ref.shape[1], tiles_ref.shape[2]
+    part = slots // PARTS
+    row_tiles = x_ref.shape[1] // tile
+    by_distance = [sorted(range(lines), key=lambda o: (abs(o - l), o)) for l in range(lines)]
+
+    def spot_of(j):
+        spot = jnp.int32(0)
+        for l in range(lines):
+            spot = jnp.where(line == l, by_distance[l][j], spot)
+        return spot
+
+    jobs = [("along", 0)]
+    for step in range(2, lines):
+        jobs += [("along", step - 1), ("across", step - 2)]
+    jobs += [("across", lines - 2), ("along", lines - 1), ("across", lines - 1)]
+    sources = [spot_of(j) * 2 + (side if kind == "along" else 1 - side) for kind, j in jobs]
+
+    def tile_copy(n):
+        job, q = n // PARTS, n % PARTS
+        return pltpu.make_async_copy(
+            tiles_ref.at[sources[job], pl.ds(q * part, part)], tile_buf.at[n % DEEP], tile_sems.at[n % DEEP]
+        )
+
+    def stage(job):
+        kind, j = jobs[job]
+        b = sources[job]
+        target = along if kind == "along" else across_buf
         for c in range(CHUNKS):
-            sends(act, c, blk, has_low, has_high, True, own=True)
-        for step in range(1, lines):
-            for c in range(CHUNKS):
-                for above in (True, False):
-                    spot = line + step if above else line - step
-                    b = spot * 2 + side
-
-                    @pl.when(spot < lines if above else spot >= 0)
-                    def _(b=b, above=above, c=c):
-                        if wait:
-                            arrive(b, c)
-                        across = True if c >= half else b != mate_block
-                        sends(act, c, b, has_low if above else None, None if above else has_high, across)
-            if step == 1:
-                for c in range(half):
-                    if wait:
-                        arrive(partner, c)
-                    extra(act, c)
-
-    own_copies = [
-        pltpu.make_async_copy(x_ref, all_ref.at[blk], own_sems.at[0]),
-        pltpu.make_async_copy(w_ref, wall_ref.at[pl.ds(feat * w_rows, w_rows), :], own_sems.at[1]),
-    ]
-    for own in own_copies:
-        own.start()
+            if kind == "across" and (j > 0 or c >= half):
+                arrive(b, c)
+
+        @pl.loop(0, row_tiles)
+        def _(t):
+            lanes = pl.ds(pl.multiple_of(t * tile, tile), tile)
+            target[t] = x_ref[:, lanes] if job == 0 else all_ref[b, :, lanes]
+
+    total_parts = len(jobs) * PARTS
+
+    def multiply(job, q):
+        n = job * PARTS + q
+        b = sources[job]
+        if q == 0:
+            stage(job)
+        src = along if jobs[job][0] == "along" else across_buf
+        tile_copy(n).wait()
+
+        @pl.loop(0, part // GROUP)
+        def _(g):
+            products = []
+            for i in range(GROUP):
+                k = g * GROUP + i
+                products.append(
+                    lax.dot_general(
+                        src[meta_ref[b, slots + q * part + k]], tile_buf[n % DEEP, k], (((1,), (1,)), ((), ())),
+                        preferred_element_type=jnp.float32,
+                    )
+                )
+            for i in range(GROUP):
+                k = q * part + g * GROUP + i
+                sums[row_tiles + k] = sums[meta_ref[b, k]] + products[i]
+
+        if n + DEEP < total_parts:
+            tile_copy(n + DEEP).start()
+        if q == PARTS - 1 and job < len(jobs) - 1:
+            @pl.loop(0, row_tiles)
+            def _(r):
+                sums[r] = sums[meta_ref[b, 2 * slots + r]]
+
+    own_copy = pltpu.make_async_copy(w_ref, wall_ref.at[pl.ds(feat * w_rows, w_rows), :], own_sems.at[0])
+    own_copy.start()
+    for n in range(DEEP):
+        tile_copy(n).start()
+    for c in range(CHUNKS):
+        sends(lambda d: d.start(), c, blk, has_low, has_high, True, own=True)
     for k in range(1, n_feat):
         weight_copy(k).start()
-    plan(lambda d: d.start(), True)
-    for c in range(half, CHUNKS):
-        arrive(partner, c)
+    scale = 1.0 + eps_ref[0]
+    for r in range(row_tiles):
+        sums[r] = scale * x_ref[:, r * tile : (r + 1) * tile].astype(jnp.float32)
+    for q in range(PARTS):
+        multiply(0, q)
     for step in range(1, lines):
-        spot = lax.rem(line + step, lines)
         for c in range(CHUNKS):
-            arrive(spot * 2 + (1 - side), c)
+            if step > 1:
+                lo = c * 2 * PARTS // CHUNKS
+                for u in range(lo, (c + 1) * 2 * PARTS // CHUNKS):
+                    multiply(1 + 2 * (step - 2) + u // PARTS, u % PARTS)
+            relay(lambda d: d.start(), True, step, c)
+        if step == 1:
+            for c in range(half):
+                arrive(partner, c)
+                extra(lambda d: d.start(), c)
+    for job in range(len(jobs) - 3, len(jobs)):
+        for q in range(PARTS):
+            multiply(job, q)
+    for r in range(row_tiles):
+        comb_ref[:, r * tile : (r + 1) * tile] = sums[meta_ref[sources[-1], 2 * slots + r]].astype(comb_ref.dtype)
     for k in range(1, n_feat):
         weight_arrive(k)
-    plan(lambda d: d.wait_send(), False)
+    for c in range(CHUNKS):
+        sends(lambda d: d.wait_send(), c, blk, has_low, has_high, True, own=True)
+    for step in range(1, lines):
+        for c in range(CHUNKS):
+            relay(lambda d: d.wait_send(), False, step, c)
+    for c in range(half):
+        extra(lambda d: d.wait_send(), c)
     for k in range(1, n_feat):
         weight_copy(k).wait_send()
-    for own in own_copies:
-        own.wait()
-
-
-def gather_all(lines, n_feat, x_t, w_pack):
+    own_copy.wait()
+
+
+def gather_aggregate(lines, n_feat, x_t, w_pack, meta, eps_self, tile_values):
     feats, rows = x_t.shape
-    blocks = lines * 2
+    blocks, slots, tile, _ = tile_values.shape
+    row_tiles = rows // tile
     return pl.pallas_call(
         functools.partial(gather_kernel, lines, n_feat),
         out_shape=(
-            jax.ShapeDtypeStruct((blocks, feats, rows), x_t.dtype),
+            jax.ShapeDtypeStruct((feats, rows), x_t.dtype),
             jax.ShapeDtypeStruct((n_feat * w_pack.shape[0], w_pack.shape[1]), w_pack.dtype),
         ),
-        in_specs=[pl.BlockSpec(memory_space=pltpu.VMEM)] * 2,
-        out_specs=(pl.BlockSpec(memory_space=pl.ANY), pl.BlockSpec(memory_space=pltpu.VMEM)),
+        in_specs=[
+            pl.BlockSpec(memory_space=pltpu.VMEM),
+            pl.BlockSpec(memory_space=pltpu.VMEM),
+            pl.BlockSpec(memory_space=pltpu.SMEM),
+            pl.BlockSpec(memory_space=pltpu.SMEM),
+            pl.BlockSpec(memory_space=pl.ANY),
+        ],
+        out_specs=(pl.BlockSpec(memory_space=pltpu.VMEM), pl.BlockSpec(memory_space=pltpu.VMEM)),
         scratch_shapes=[
+            pltpu.VMEM((blocks, feats, rows), x_t.dtype),
+            pltpu.VMEM((row_tiles, feats, tile), x_t.dtype),
+            pltpu.VMEM((row_tiles, feats, tile), x_t.dtype),
+            pltpu.VMEM((DEEP, slots // PARTS, tile, tile), tile_values.dtype),
+            pltpu.VMEM((row_tiles + slots, feats, tile), jnp.float32),
             pltpu.SemaphoreType.DMA((3, blocks, CHUNKS)),
             pltpu.SemaphoreType.DMA((blocks, CHUNKS)),
             pltpu.SemaphoreType.DMA((n_feat - 1,)),
             pltpu.SemaphoreType.DMA((n_feat - 1,)),
-            pltpu.SemaphoreType.DMA((2,)),
+            pltpu.SemaphoreType.DMA((1,)),
+            pltpu.SemaphoreType.DMA((DEEP,)),
         ],
         compiler_params=pltpu.CompilerParams(
             collective_id=0, has_side_effects=True, vmem_limit_bytes=VMEM_LIMIT
         ),
-    )(x_t, w_pack)
-
-
-def aggregate_kernel(group, rows_ref, cols_ref, eps_ref, x_ref, tiles_ref, own_ref, out_ref, acc):
-    src = pl.program_id(0)
-    slots, tile = tiles_ref.shape[1], tiles_ref.shape[2]
-
-    @pl.when(src == 0)
-    def _():
-        acc[...] = jnp.zeros_like(acc)
-
-    @pl.loop(0, slots // group)
-    def _(g):
-        products = []
-        for i in range(group):
-            k = g * group + i
-            lanes = pl.ds(pl.multiple_of(cols_ref[src, k] * tile, tile), tile)
-            products.append(
-                lax.dot_general(
-                    x_ref[0, :, lanes], tiles_ref[0, k], (((1,), (1,)), ((), ())),
-                    preferred_element_type=jnp.float32,
-                )
-            )
-        for i in range(group):
-            r = rows_ref[src, g * group + i]
-            acc[r] = acc[r] + products[i]
-
-    @pl.when(src == pl.num_programs(0) - 1)
-    def _():
-        scale = 1.0 + eps_ref[0]
-        for r in range(acc.shape[0]):
-            lanes = pl.ds(r * tile, tile)
-            own = own_ref[:, lanes].astype(jnp.float32)
-            out_ref[:, lanes] = (scale * own + acc[r]).astype(out_ref.dtype)
-
-
-def aggregate(x_all, tile_rows, tile_cols, tile_values, eps_self, x_t):
-    blocks, slots, tile, _ = tile_values.shape
-    feats, rows = x_t.shape
-    group = 8 if slots % 8 == 0 else 1
-    return pl.pallas_call(
-        functools.partial(aggregate_kernel, group),
-        out_shape=jax.ShapeDtypeStruct((feats, rows), x_t.dtype),
-        grid_spec=pltpu.PrefetchScalarGridSpec(
-            num_scalar_prefetch=3,
-            grid=(blocks,),
-            in_specs=[
-                pl.BlockSpec((1, feats, rows), lambda s, *_: (s, 0, 0)),
-                pl.BlockSpec((1, slots, tile, tile), lambda s, *_: (s, 0, 0, 0)),
-                pl.BlockSpec((feats, rows), lambda s, *_: (0, 0)),
-            ],
-            out_specs=pl.BlockSpec((feats, rows), lambda s, *_: (0, 0)),
-            scratch_shapes=[pltpu.VMEM((rows // tile, feats, tile), jnp.float32)],
-        ),
-        compiler_params=pltpu.CompilerParams(vmem_limit_bytes=VMEM_LIMIT),
-    )(tile_rows, tile_cols, eps_self, x_all, tile_values, x_t)
+    )(x_t, w_pack, meta, eps_self, tile_values)
+
+
+def chain_meta(tile_rows, tile_cols, row_tiles):
+    slots = tile_rows.shape[1]
+    slot = jnp.arange(slots, dtype=jnp.int32)
+    same = tile_rows[:, :, None] == tile_rows[:, None, :]
+    earlier = jnp.max(jnp.where(same & (slot[None, None, :] < slot[None, :, None]), slot[None, None, :], -1), axis=2)
+    prev = jnp.where(earlier >= 0, row_tiles + earlier, tile_rows)
+    row = jnp.arange(row_tiles, dtype=jnp.int32)
+    hit = tile_rows[:, None, :] == row[None, :, None]
+    final = jnp.max(jnp.where(hit, slot[None, None, :], -1), axis=2)
+    last = jnp.where(final >= 0, row_tiles + final, row[None, :])
+    return jnp.concatenate([prev, tile_cols, last], axis=1)
 
 
 def perceptron_kernel(n_feat, comb_ref, w_ref, out_ref, rows_in, staged, in_send, in_recv, out_send, out_recv, own_sems):
@@ -337,8 +392,8 @@
         biases = jnp.stack([b_one, b_two], axis=1)
         biases = jnp.pad(biases, ((0, 0), (0, tile_values.shape[2] - 2)))
         w_pack = jnp.concatenate([w_one.T, w_two, biases], axis=1)
-        x_all, w_all = gather_all(lines, n_feat, x_t, w_pack)
-        comb_t = aggregate(x_all, tile_rows, tile_cols, tile_values, eps_self, x_t)
+        meta = chain_meta(tile_rows, tile_cols, x_t.shape[1] // tile_values.shape[2])
+        comb_t, w_all = gather_aggregate(lines, n_feat, x_t, w_pack, meta, eps_self, tile_values)
         return perceptron(n_feat, comb_t, w_all).T
 
     return jax.shard_map(

time: 171 us -> 142 us (0.83)
  Pallas kernels: 165 us -> 133 us
  other arithmetic: 2.1 us -> 6.13 us
    pallas_call x2 -> x1, Pallas kernels: 136 us -> 104 us  [gather_aggregate(): pl.pallas_call(functools.partial(gather_kernel, lines, n_feat), out_shape...]
    reduce_max x0 -> x2, other arithmetic: none -> 2.03 us  [the longest x1 1.13 us: chain_meta(): jnp.max(jnp.where(same & (slot[None, None, :] < slot[None, :, None]), slo...]
where the time goes in v2:
time: 142 us
  Pallas kernels  133 us (94%)
  other arithmetic  6.13 us (4%)
  local copies, waits for them, and re-layouts  2.38 us (2%)
    pallas_call x1, Pallas kernels, gather_aggregate(): pl.pallas_call(functools.partial(gather_kernel, lines, n_feat), out_shape...  104 us
    pallas_call x1, Pallas kernels, perceptron(): pl.pallas_call(functools.partial(perceptron_kernel, n_feat), out_shape=ja...  28.7 us

profile of v2, /device:TPU:1, one launch (start us, length us, event | category | flops | bytes accessed | tf_op | source)
XLA Modules:
  0.0 142.0 jit_solution(3274106001595789505)
XLA Ops:
  0.7 0.7 pad_maximum_fusion
  1.3 0.9 select_reduce_fusion.1
  2.2 0.1 copy.13
  2.4 1.1 select_reduce_fusion
  3.5 0.7 add_select_fusion
  4.2 1.3 pad_add_fusion.meta_ref
  5.5 1.4 fusion.1.w_ref
  6.9 104.1 %shard_map.91 = (bf16[64,8192]{1,0:T(8,128)(2,1)}, bf16[256,640]{1,0:T(8,128)(2,1)}) custom-call(bf16[64,8192]{1,0:T(8,128)(2,1)} %bitcast.6, bf16[64,640]{1,0:T(8,128)(2,1)} %fusion.1.w_ref, s32[8,320]{1,0:T(8,128)} %pad_add_fusion.meta_ref, f32[1]{0:T(128)S(6)} %copy.15.eps_ref, bf16[8,128,128,128]{3,2,1,0:T(8,128)(2,1)} %tiles_ref.1), custom_call_target="tpu_custom_call" | custom-call | tf_op jit(solution)/shard_map/pallas_call | solution.py:239
  111.0 28.7 %shard_map.92 = bf16[64,8192]{1,0:T(8,128)(2,1)} custom-call(bf16[64,8192]{1,0:T(8,128)(2,1)} %get-tuple-element.7.comb_ref, bf16[256,640]{1,0:T(8,128)(2,1)} %get-tuple-element.8.w_ref), custom_call_target="tpu_custom_call" | custom-call | tf_op jit(solution)/shard_map/pallas_call | solution.py:370
  139.7 2.3 %copy.16 = bf16[8192,64]{0,1:T(8,128)(2,1)} copy(bf16[8192,64]{0,1:T(8,128)(2,1)} %bitcast.5) | data formatting | bytes 2097152
  (2 shorter events, 0.0 us)

commit v3 on v2

--- a/solution.py
+++ b/solution.py
@@ -202,20 +202,25 @@
         sums[r] = scale * x_ref[:, r * tile : (r + 1) * tile].astype(jnp.float32)
     for q in range(PARTS):
         multiply(0, q)
+    done = PARTS
     for step in range(1, lines):
         for c in range(CHUNKS):
-            if step > 1:
-                lo = c * 2 * PARTS // CHUNKS
-                for u in range(lo, (c + 1) * 2 * PARTS // CHUNKS):
-                    multiply(1 + 2 * (step - 2) + u // PARTS, u % PARTS)
+            if step == lines - 1 and step > 1:
+                before = (2 * step - 3) * PARTS + 3 * PARTS // 2
+                upto = before + c * (3 * PARTS // 2) // (CHUNKS - 1)
+            else:
+                upto = (2 * step - 3) * PARTS + (c + 1) * 2 * PARTS // CHUNKS
+            while done < upto:
+                multiply(done // PARTS, done % PARTS)
+                done += 1
             relay(lambda d: d.start(), True, step, c)
         if step == 1:
             for c in range(half):
                 arrive(partner, c)
                 extra(lambda d: d.start(), c)
-    for job in range(len(jobs) - 3, len(jobs)):
-        for q in range(PARTS):
-            multiply(job, q)
+    while done < total_parts:
+        multiply(done // PARTS, done % PARTS)
+        done += 1
     for r in range(row_tiles):
         comb_ref[:, r * tile : (r + 1) * tile] = sums[meta_ref[sources[-1], 2 * slots + r]].astype(comb_ref.dtype)
     for k in range(1, n_feat):

time: 142 us -> 138 us (0.972)
  Pallas kernels: 133 us -> 128 us
    pallas_call x1, Pallas kernels: 104 us -> 99.2 us  [gather_aggregate(): pl.pallas_call(functools.partial(gather_kernel, lines, n_feat), out_shape...]
where the time goes in v3:
time: 138 us
  Pallas kernels  128 us (93%)
  other arithmetic  6.13 us (4%)
  local copies, waits for them, and re-layouts  2.38 us (2%)
    pallas_call x1, Pallas kernels, gather_aggregate(): pl.pallas_call(functools.partial(gather_kernel, lines, n_feat), out_shape...  99.2 us
    pallas_call x1, Pallas kernels, perceptron(): pl.pallas_call(functools.partial(perceptron_kernel, n_feat), out_shape=ja...  29.2 us

profile of v3, /device:TPU:1, one launch (start us, length us, event | category | flops | bytes accessed | tf_op | source)
XLA Modules:
  0.0 137.6 jit_solution(18101171456950015082)
XLA Ops:
  0.7 0.7 pad_maximum_fusion
  1.3 0.9 select_reduce_fusion.1
  2.2 0.1 copy.13
  2.4 1.1 select_reduce_fusion
  3.5 0.7 add_select_fusion
  4.2 1.3 pad_add_fusion.meta_ref
  5.5 1.4 %fusion.1.w_ref = bf16[64,640]{1,0:T(8,128)(2,1)} fusion(bf16[64,2]{1,0:T(8,128)(2,1)S(1)} %copy.13, bf16[64,256]{1,0:T(8,128)(2,1)} %param.16, bf16[64,256]{1,0:T(8,128)(2,1)} %bitcast.7), kind=kLoop, calls=%fused_computation.5 | loop fusion | flops 327680 | bytes 147712 | tf_op jit(solution)/shard_map/concatenate | solution.py:399
  6.9 99.2 %shard_map.91 = (bf16[64,8192]{1,0:T(8,128)(2,1)}, bf16[256,640]{1,0:T(8,128)(2,1)}) custom-call(bf16[64,8192]{1,0:T(8,128)(2,1)} %bitcast.6, bf16[64,640]{1,0:T(8,128)(2,1)} %fusion.1.w_ref, s32[8,320]{1,0:T(8,128)} %pad_add_fusion.meta_ref, f32[1]{0:T(128)S(6)} %copy.15.eps_ref, bf16[8,128,128,128]{3,2,1,0:T(8,128)(2,1)} %tiles_ref.1), custom_call_target="tpu_custom_call" | custom-call | tf_op jit(solution)/shard_map/pallas_call | solution.py:244
  106.1 29.2 %shard_map.92 = bf16[64,8192]{1,0:T(8,128)(2,1)} custom-call(bf16[64,8192]{1,0:T(8,128)(2,1)} %get-tuple-element.7.comb_ref, bf16[256,640]{1,0:T(8,128)(2,1)} %get-tuple-element.8.w_ref), custom_call_target="tpu_custom_call" | custom-call | tf_op jit(solution)/shard_map/pallas_call | solution.py:375
  135.4 2.3 %copy.16 = bf16[8192,64]{0,1:T(8,128)(2,1)} copy(bf16[8192,64]{0,1:T(8,128)(2,1)} %bitcast.5) | data formatting | bytes 2097152
  (2 shorter events, 0.0 us)
